TPU v7x, 32 devices: a whole 2x2x4 slice. The times are simulated.
32 devices in a mesh: expert: 4 (over y, x), rep: 4 (over z), hid: 2 (over core).
Axes of the slice: x: 2, y: 2, z: 4, core: 2. Of those that a mesh axis runs over, the one named last changes fastest.
Arguments:
- calib_rows: bfloat16 [8192, 6144], P(('expert', 'rep'), 'hid'), may hold values from -6 to 6
- routes: int32 [8192, 2], P(('expert', 'rep')), may hold values from 0 to 7, all different within a row; in each aligned block of 512 rows (0 to 511, 512 to 1023, ...) at most 256 rows name the same one
- sketch_seed: int32 [6144, 512], P('hid'), may hold values from -1 to 1
- up_weight: bfloat16 [8, 6144, 16384], P('expert', 'hid', 'rep'), may hold values from -0.078125 to 0.078125
Outputs:
- projected: float32 [16384, 8, 512], P(('rep', 'hid'), 'expert')
Inputs may be any that keep to these rules, and one draw needn't show every extreme that they name: `routes`: each row names 2 different experts. In each aligned block of 512 rows no expert is named by more than 256 rows, and every expert is named somewhere.
All inputs are finite; a program needn't handle non-finite values.
Results may differ from a plain program's by a relative error of at most 0.0037.
Values may be sent and summed in bfloat16 or wider, within the bound.
No kernel may reach another device: no remote copies, remote signals or barrier semaphores. Data moves between devices by JAX's collectives and lax.ppermute only.
A program may use at most 192 MiB of HBM per device.

v0:
```python
import jax
import jax.numpy as jnp
from jax import lax
from jax.sharding import PartitionSpec as P

D = 6144
EXPERTS = 8
CAP = 256


damping = 0.25


def shards(calib_rows, routes, sketch_seed, up_weight):
    exp_local = up_weight.shape[0]
    signs_half = sketch_seed.astype(jnp.bfloat16)
    signs_full = sketch_seed.astype(jnp.float32)
    expert_ids = jnp.arange(EXPERTS, dtype=jnp.int32)
    member = jnp.sum((routes[:, :, None] == expert_ids[None, None, :]).astype(jnp.float32), axis=1)
    row_squares = jnp.sum(jnp.square(calib_rows.astype(jnp.float32)), axis=1)
    leader = (lax.axis_index("hid") == 0).astype(jnp.float32)
    counts, squares = lax.psum(
        (jnp.sum(member, axis=0) * leader, jnp.sum(member * row_squares[:, None], axis=0)),
        ("expert", "rep", "hid"),
    )
    flat_routes = routes.reshape(-1)
    one_hot = (flat_routes[:, None] == expert_ids[None, :]).astype(jnp.int32)
    before = jnp.cumsum(one_hot, axis=0) - one_hot
    slot_index = jnp.sum(before * one_hot, axis=1)
    repeated = jnp.repeat(calib_rows, routes.shape[1], axis=0)
    outgoing = jnp.zeros((EXPERTS, CAP, calib_rows.shape[1]), jnp.bfloat16)
    outgoing = outgoing.at[flat_routes, slot_index].set(repeated)
    outgoing = outgoing.reshape(lax.axis_size("expert"), exp_local, CAP, calib_rows.shape[1])
    rows_here = lax.all_to_all(outgoing, "expert", split_axis=0, concat_axis=2, tiled=True)[0]
    partial_value = jnp.einsum(
        "kmd,dr->kmr", rows_here, signs_half, preferred_element_type=jnp.float32
    )
    summed_rows = lax.psum(partial_value, "hid")
    masked = summed_rows.astype(jnp.bfloat16)
    partial_gram = jnp.einsum("kmd,kmr->kdr", rows_here, masked, preferred_element_type=jnp.float32)
    summed = lax.psum(partial_gram, "rep")
    first_expert = lax.axis_index("expert") * exp_local
    row_counts = lax.dynamic_slice_in_dim(counts, first_expert, exp_local)
    square_sums = lax.dynamic_slice_in_dim(squares, first_expert, exp_local)
    ridge = damping * square_sums / (row_counts * D)
    sketch = (
        summed / row_counts[:, None, None] + ridge[:, None, None] * signs_full[None, :, :]
    ).astype(jnp.bfloat16)
    return lax.psum_scatter(
        jnp.einsum("edf,edr->fer", up_weight, sketch, preferred_element_type=jnp.float32),
        "hid",
        scatter_dimension=0,
        tiled=True,
    )


def solution(mesh):
    in_specs = (
        P(("expert", "rep"), "hid"),
        P(("expert", "rep"), None),
        P("hid", None),
        P("expert", "hid", "rep"),
    )
    out_specs = P(("rep", "hid"), "expert", None)
    return jax.shard_map(shards, mesh=mesh, in_specs=in_specs, out_specs=out_specs, check_vma=False)
```

profile of v0, /device:TPU:0, one launch (start us, length us, event | category | flops | bytes accessed | tf_op | source)
XLA Modules:
  0.0 748.2 jit_solution(2252918654287226031)
XLA Ops:
  6.5 0.8 copy.22
  7.7 0.2 reshape.73
  7.9 2.3 reduce-window.6
  10.2 0.3 slice_reduce_fusion
  10.7 0.8 and_reduce_fusion
  11.5 0.7 multiply_reduce_fusion.2
  12.2 7.0 broadcast_in_dim.5
  19.3 13.6 %reshape.84 = bf16[1024,3072]{1,0:T(8,128)(2,1)} reshape(bf16[512,2,3072]{2,1,0:T(2,128)(2,1)} %broadcast_in_dim.5) | data formatting | bytes 12582912 | tf_op jit(solution)/shard_map/reshape | solution.py:30
  32.9 17.2 %scatter_custom_fusion = bf16[2048,3072]{1,0:T(8,128)(2,1)} fusion(s32[1024]{0:T(1024)S(1)} %broadcast_select_fusion, bf16[1024,3072]{1,0:T(8,128)(2,1)} %reshape.84, bf16[]{:T(256)} %constant.10.clone.1), kind=kCustom, calls=%fused_computation.3 | custom fusion | bytes 12583424
  50.0 144.0 %all_to_all.15 = bf16[4,2,256,3072]{3,2,1,0:T(8,128)(2,1)S(1)} all-to-all(bf16[4,2,256,3072]{3,2,1,0:T(8,128)(2,1)} %bitcast.35), channel_id=1, replica_groups=mesh['expert'=4,'rep'=4,'hid'=2] {'expert'}, dimensions={0} | all-to-all | bytes 25165824 | tf_op jit(solution)/shard_map/all_to_all | solution.py:34
  194.0 2.3 copy.25
  196.3 4.5 copy-done
  200.8 8.8 %fusion.5 = f32[2,1024,512]{2,1,0:T(8,128)} fusion(bf16[2,1024,3072]{2,1,0:T(8,128)(2,1)S(1)} %bitcast.37, s32[3072,512]{1,0:T(8,128)S(1)} %bitcast.40), kind=kOutput, calls=%fused_computation.9 | convolution fusion | flops 6444023808 | bytes 23068672 | tf_op jit(solution)/shard_map/kmd,dr->kmr/dot_general | solution.py:35
  209.6 14.9 %all-reduce.5 = bf16[2,1024,512]{2,1,0:T(8,128)(2,1)S(1)} all-reduce(f32[2,1024,512]{2,1,0:T(8,128)} %fusion.5), channel_id=1, replica_groups=mesh['expert'=4,'rep'=4,'hid'=2] {'hid'}, use_global_device_ids=true, to_apply=%region_4.0 | all-reduce | flops 1048576 | bytes 6291456 | tf_op jit(solution)/shard_map/psum | solution.py:38
  224.5 12.4 %fusion.14 = f32[2,3072,512]{2,1,0:T(8,128)} fusion(bf16[2,1024,3072]{2,1,0:T(8,128)(2,1)} %bitcast.38, bf16[2,1024,512]{2,1,0:T(8,128)(2,1)S(1)} %all-reduce.5), kind=kOutput, calls=%fused_computation.35 | convolution fusion | flops 6442450944 | bytes 27262976 | tf_op jit(solution)/shard_map/kmd,kmr->kdr/dot_general | solution.py:40
  237.0 0.6 copy-done.2
  237.7 1.1 copy-done.1
  238.8 0.7 multiply_reduce_fusion
  239.6 44.5 %all-reduce = (f32[8]{0:T(128)S(1)}, f32[8]{0:T(128)S(1)}) all-reduce(f32[8]{0:T(128)S(1)} %broadcast_multiply_fusion, f32[8]{0:T(128)S(1)} %multiply_reduce_fusion.1), channel_id=1, replica_groups=mesh['expert'=4,'rep'=4,'hid'=2] {'expert','rep','hid'}, use_global_device_ids=true, to_apply=%region_7.8 | all-reduce | flops 16 | bytes 128 | tf_op jit(solution)/shard_map/psum | solution.py:22
  284.1 6.3 convert_element_type.35
  290.4 373.7 %all-reduce.4.cloned.1.call-done = f32[2,3072,512]{2,1,0:T(8,128)} async-done(((f32[2,3072,512]{2,1,0:T(8,128)}), f32[2,3072,512]{2,1,0:T(8,128)}) %all-reduce.4.cloned.1.call-update) | async-done | bytes 12582928 | tf_op jit(solution)/shard_map/psum | solution.py:41
  664.2 40.0 %convolution_bitcast_fusion = f32[4096,2,512]{0,2,1:T(8,128)} fusion(bf16[2,3072,4096]{2,1,0:T(8,128)(2,1)} %param.7, f32[2,3072,512]{2,1,0:T(8,128)} %all-reduce.4.cloned.1.call-done, f32[3072,512]{1,0:T(8,128)} %convert_element_type.35, f32[2]{0:T(128)S(1)} %get-tuple-element.9, f32[2]{0:T(128)S(1)} %get-tuple-element.10), kind=kOutput, calls=%fused_computation.2 | convolution fusion | flops 25782386688 | bytes 85983248 | tf_op jit(solution)/shard_map/edf,edr->fer/dot_general | solution.py:50
  704.2 24.0 %reduce-scatter.2.cloned.1.call-done = f32[2048,2,512]{0,2,1:T(8,128)} async-done(((f32[4096,2,512]{0,2,1:T(8,128)}), f32[2048,2,512]{0,2,1:T(8,128)}) %reduce-scatter.2.cloned.1.call-update) | async-done | bytes 8388624 | tf_op jit(solution)/shard_map/reduce_scatter | solution.py:49
  728.2 13.1 %copy.28 = f32[2048,2,512]{2,1,0:T(2,128)} copy(f32[2048,2,512]{0,2,1:T(8,128)} %reduce-scatter.2.cloned.1.call-done) | data formatting | bytes 16777216 | tf_op jit(solution)/shard_map/reduce_scatter | solution.py:49
  (24 shorter events, 1.0 us)
Async XLA Ops:
  6.5 657.6 %all-reduce.4.cloned.1.call-start = ((), (), s32[]{:S(2)}) async-start(), calls=%async_computation.2 | async-start | bytes 25165824 | tf_op jit(solution)/shard_map/psum | solution.py:41
  50.0 150.7 %slice-start = ((s8[6291456]{0:T(1024)(128)(4,1)}), s8[4194304]{0:T(1024)(128)(4,1)S(1)}, s32[]{:S(2)}) async-start(s8[6291456]{0:T(1024)(128)(4,1)} %bitcast.39), calls=%async_computation.4 | async-start | bytes 8388608
  194.0 6.8 slice-start.1
  196.3 4.5 copy-start
  236.9 0.7 copy-start.2
  236.9 1.9 copy-start.1
  236.9 491.3 %reduce-scatter.2.cloned.1.call-start = ((), (), s32[]{:S(2)}) async-start(), calls=%async_computation.3 | async-start | bytes 25165824 | tf_op jit(solution)/shard_map/reduce_scatter | solution.py:49
Sparse Core Ops, SparseCore 0:
  237.0 427.0 all-reduce.3
  704.3 23.8 reduce-scatter.1
where the time goes:
time: 749 us; the launch traced here: 748 us
  waiting for transfers between devices  398 us (53%)
  blocking collectives  203 us (27%)
  matrix products  61.1 us (8%)
  local copies, waits for them, and re-layouts  61 us (8%)
  between operations  13.5 us (2%)
  other arithmetic  11.3 us (2%)
    psum x1, waiting for transfers between devices, shards(): summed = lax.psum(partial_gram, 'rep')  374 us
    all_to_all x1, blocking collectives, shards(): lax.all_to_all(outgoing, 'expert', split_axis=0, concat_axis=2, tiled=True)  144 us
    psum x1, blocking collectives, shards(): lax.psum((jnp.sum(member, axis=0) * leader, jnp.sum(member * row_squares[...  44.5 us
    dot_general x1, matrix products, shards(): jnp.einsum('edf,edr->fer', up_weight, sketch, preferred_element_type=jnp....  40 us
    unnamed x12, local copies, waits for them, and re-layouts  24.1 us
    reduce_scatter x1, waiting for transfers between devices, shards(): lax.psum_scatter(jnp.einsum('edf,edr->fer', up_weight, sketch, preferred_...  24 us
  transfers between devices with their start and end apart: 2, of which 2 were waited for; matrix products, arithmetic and copies ran while one was open for 1% of the time, Pallas kernels for 0%

commit v1 on v0

v1 whole, which is shorter than its diff:
```python
import math

import jax
import jax.numpy as jnp
from jax import lax
from jax.experimental import pallas as pl
from jax.experimental.pallas import tpu as pltpu
from jax.sharding import PartitionSpec as P


D = 6144
EXPERTS = 8
EXTRA = 16
damping = 0.25


def split3(value):
    hi = lax.reduce_precision(value, 8, 7)
    mid = lax.reduce_precision(value - hi, 8, 7)
    return jnp.stack([hi, mid, value - hi - mid])


def flip_kernel(x_ref, extra_ref, p_ref, *, d):
    flipped = x_ref[...].T
    for g in range(p_ref.shape[0]):
        p_ref[g, :d, :] = flipped[g * d : (g + 1) * d, :]
        p_ref[g, d:, :] = extra_ref[...]


def flip(calib_rows, extra, chips):
    tokens, local = calib_rows.shape
    d = local // chips
    group = 128 // math.gcd(d, 128)
    if d % 16 or chips % group:
        return jnp.concatenate(
            [
                calib_rows.T.reshape(chips, d, tokens),
                jnp.broadcast_to(extra[None], (chips, EXTRA, tokens)),
            ],
            axis=1,
        )
    return pl.pallas_call(
        lambda *refs: flip_kernel(*refs, d=d),
        out_shape=jax.ShapeDtypeStruct((chips, d + EXTRA, tokens), jnp.bfloat16),
        grid=(chips // group,),
        in_specs=[
            pl.BlockSpec((tokens, group * d), lambda j: (0, j)),
            pl.BlockSpec((EXTRA, tokens), lambda j: (0, 0)),
        ],
        out_specs=pl.BlockSpec((group, d + EXTRA, tokens), lambda j: (j, 0, 0)),
        cost_estimate=pl.CostEstimate(
            flops=tokens * local, bytes_accessed=4 * tokens * local, transcendentals=0
        ),
        name="flip",
    )(calib_rows, extra)


def gram_kernel(counts_ref, ridge_ref, x_ref, m_ref, s_ref, o_ref, lhs, acc, *, which, per, d):
    step = pl.program_id(0)
    groups = o_ref.shape[0]
    sources, _, tokens = x_ref.shape
    for s in range(sources):
        x = x_ref[s, :d, :]
        for g in range(groups):
            row = d + g * per + which
            lhs[g, :, s * tokens : (s + 1) * tokens] = x * x_ref[s, row : row + 1, :]
    flat = lhs[...].reshape(groups * d, sources * tokens)
    rows = m_ref[...].reshape(sources * tokens, m_ref.shape[-1])
    part = jnp.dot(flat, rows, preferred_element_type=jnp.float32)

    @pl.when(step == 0)
    def _():
        acc[...] = part

    @pl.when(step > 0)
    def _():
        acc[...] += part

    @pl.when(step == pl.num_programs(0) - 1)
    def _():
        signs = s_ref[...].astype(jnp.float32)
        for g in range(groups):
            e = g * per + which
            total = acc[g * d : (g + 1) * d, :]
            o_ref[g] = (total / counts_ref[e] + ridge_ref[e] * signs).astype(jnp.bfloat16)


def gram(counts, ridge, received, sketched, signs, which, per):
    sources, rows, tokens = received.shape
    d = rows - EXTRA
    batch, hid, _, share, width = sketched.shape
    groups = EXPERTS // per
    return pl.pallas_call(
        lambda *refs: gram_kernel(*refs, which=which, per=per, d=d),
        out_shape=jax.ShapeDtypeStruct((groups, d, width), jnp.bfloat16),
        grid=(sources // batch,),
        in_specs=[
            pl.BlockSpec(memory_space=pltpu.SMEM),
            pl.BlockSpec(memory_space=pltpu.SMEM),
            pl.BlockSpec((batch, rows, tokens), lambda j: (j, 0, 0)),
            pl.BlockSpec((batch, hid, 1, share, width), lambda j: (0, 0, j, 0, 0)),
            pl.BlockSpec((d, width), lambda j: (0, 0)),
        ],
        out_specs=pl.BlockSpec((groups, d, width), lambda j: (0, 0, 0)),
        scratch_shapes=[
            pltpu.VMEM((groups, d, batch * tokens), jnp.bfloat16),
            pltpu.VMEM((groups * d, width), jnp.float32),
        ],
        cost_estimate=pl.CostEstimate(
            flops=2 * sources * groups * d * tokens * width,
            bytes_accessed=2 * sources * tokens * (rows + width),
            transcendentals=0,
        ),
        name="gram",
    )(counts, ridge, received, sketched, signs)


def weave_kernel(*refs):
    fresh_ref, away_ref, o_ref = refs[-3], refs[-2], refs[-1]
    done = refs[:-3]
    for k, ref in enumerate(done):
        o_ref[:, k, :] = ref[...]
    o_ref[:, len(done), :] = fresh_ref[...] + away_ref[...]


def weave(done, fresh, away):
    block, width = fresh.shape
    per = len(done) + 1
    tile = math.gcd(block, 256)
    spec = pl.BlockSpec((tile, width), lambda i: (i, 0))
    return pl.pallas_call(
        weave_kernel,
        out_shape=jax.ShapeDtypeStruct((block, per, width), jnp.float32),
        grid=(block // tile,),
        in_specs=[spec] * (per + 1),
        out_specs=pl.BlockSpec((tile, per, width), lambda i: (i, 0, 0)),
        cost_estimate=pl.CostEstimate(
            flops=block * width, bytes_accessed=4 * block * width * (2 * per + 1), transcendentals=0
        ),
        name="weave",
    )(*done, fresh, away)


def share(rows):
    experts, hid = lax.axis_size("expert"), lax.axis_size("hid")
    if experts != 4 or hid != 2:
        rows = lax.all_gather(rows, ("expert", "hid"), axis=0, tiled=False)
        return rows.reshape(experts, hid, *rows.shape[1:])
    me, h = lax.axis_index("expert"), lax.axis_index("hid")

    def hop(value, bit):
        return lax.ppermute(value, "expert", [(p, p ^ bit) for p in range(experts)])

    def across(value):
        return lax.ppermute(value, "hid", [(0, 1), (1, 0)])

    parts = [rows] + [hop(rows, bit) for bit in range(1, experts)]
    result = jnp.zeros((experts, hid, *rows.shape), rows.dtype)
    for bit, value in enumerate(parts):
        for side, block in ((h, value), (1 - h, across(value))):
            start = (me ^ bit, side) + (0,) * rows.ndim
            result = lax.dynamic_update_slice(result, block[None, None], start)
    return result


def shards(calib_rows, routes, sketch_seed, up_weight):
    per, local, full = up_weight.shape
    tokens = calib_rows.shape[0]
    width = sketch_seed.shape[1]
    hid = lax.axis_size("hid")
    chips = lax.axis_size("rep") * lax.axis_size("expert")
    d = local // chips
    h = lax.axis_index("hid")

    ids = jnp.arange(EXPERTS, dtype=jnp.int32)
    member = jnp.sum((routes.T[:, None, :] == ids[None, :, None]).astype(jnp.float32), axis=0)
    row_squares = jnp.sum(jnp.square(calib_rows.astype(jnp.float32)), axis=1)
    squares = split3(jnp.sum(member * row_squares[None, :], axis=1))
    extra = jnp.zeros((EXTRA, tokens), jnp.float32)
    extra = extra.at[:EXPERTS].set(member)
    extra = extra.at[EXPERTS : EXPERTS + 3, :EXPERTS].set(squares).astype(jnp.bfloat16)
    pieces = flip(calib_rows, extra, chips)
    received = lax.all_to_all(pieces, ("rep", "expert"), split_axis=0, concat_axis=0, tiled=True)
    part = jnp.dot(calib_rows, sketch_seed.astype(jnp.bfloat16), preferred_element_type=jnp.float32)
    if hid == 2:
        half = tokens // 2
        mine = lax.dynamic_slice_in_dim(part, h * half, half) + lax.ppermute(
            lax.dynamic_slice_in_dim(part, (1 - h) * half, half), "hid", [(0, 1), (1, 0)]
        )
    else:
        mine = lax.psum_scatter(part, "hid", scatter_dimension=0, tiled=True)
    sketched = lax.all_gather(mine.astype(jnp.bfloat16), "rep", axis=0, tiled=False)
    sketched = share(sketched)

    stats = received[:, d:, :].astype(jnp.float32)
    counts = jnp.sum(stats[:, :EXPERTS], axis=(0, 2))
    square_sums = lax.psum(jnp.sum(stats[:, EXPERTS : EXPERTS + 3, :EXPERTS], axis=(0, 1)), "hid")
    ridge = damping * square_sums / (counts * D)
    place = lax.axis_index(("rep", "expert"))
    signs = lax.dynamic_slice_in_dim(sketch_seed, place * d, d, 0)

    block = full // hid
    swap = [(0, 1), (1, 0)]
    outs, owns = [], []
    for k in range(per):
        own = gram(counts, ridge, received, sketched, signs, k, per)
        own = lax.all_to_all(own, "expert", split_axis=0, concat_axis=0, tiled=True)
        owns.append(own.reshape(-1, width))
    sketches = []
    for k, own in enumerate(owns):
        sketches.append(lax.all_gather(own, "rep", axis=0, tiled=True))
    for k in range(per):
        sketch = lax.optimization_barrier((sketches[k], owns))[0]

        def project(start, size):
            weight = lax.dynamic_slice(up_weight, (k, 0, start), (1, local, size))[0]
            return lax.dot_general(
                weight, sketch, (((0,), (0,)), ((), ())), preferred_element_type=jnp.float32
            )

        if hid != 2:
            outs.append(
                lax.psum_scatter(project(0, full), "hid", scatter_dimension=0, tiled=True)
            )
            continue
        if outs:
            sketch, outs = lax.optimization_barrier((sketch, outs))
        away = lax.ppermute(project((1 - h) * block, block), "hid", swap)
        if k == per - 1:
            return weave(outs, project(h * block, block), away)
        outs.append(project(h * block, block) + away)
    return jnp.stack(outs, axis=1)


def solution(mesh):
    in_specs = (
        P(("expert", "rep"), "hid"),
        P(("expert", "rep"), None),
        P("hid", None),
        P("expert", "hid", "rep"),
    )
    out_specs = P(("rep", "hid"), "expert", None)

    return jax.shard_map(shards, mesh=mesh, in_specs=in_specs, out_specs=out_specs, check_vma=False)
```

time: 749 us -> 373 us (0.50)
  waiting for transfers between devices: 398 us -> 206 us
  blocking collectives: 203 us -> 19 us
  local copies, waits for them, and re-layouts: 61 us -> 20.9 us
  Pallas kernels: 0 us -> 38.4 us
  starting transfers between devices: 0.04 us -> 16.3 us
  matrix products: 61.1 us -> 50.6 us
    psum x1 -> x0, waiting for transfers between devices: 374 us -> none  [shards(): summed = lax.psum(partial_gram, 'rep')]
    all_gather x0 -> x3, waiting for transfers between devices: none -> 147 us  [the longest x2 90.8 us: shards(): sketches.append(lax.all_gather(own, 'rep', axis=0, tiled=True))]
    all_to_all x1, blocking collectives: 144 us -> 16.4 us  [shards(): own = lax.all_to_all(own, 'expert', split_axis=0, concat_axis=0, tiled=True)]
    psum x2 -> x1, blocking collectives: 59.4 us -> 2.64 us  [shards(): lax.psum(jnp.sum(stats[:, EXPERTS:EXPERTS + 3, :EXPERTS], axis=(0, 1)), '...]
    ppermute x0 -> x10, waiting for transfers between devices: none -> 48.5 us  [the longest x3 46.6 us: hop(): return lax.ppermute(value, 'expert', [(p, p ^ bit) for p in range(experts)])]
    pallas_call x0 -> x4, Pallas kernels: none -> 38.4 us  [the longest x2 21.5 us: gram(): pl.pallas_call(lambda *refs: gram_kernel(*refs, which=which, per=per, d=d...]
    reduce_scatter x1 -> x0, waiting for transfers between devices: 24 us -> none  [shards(): lax.psum_scatter(jnp.einsum('edf,edr->fer', up_weight, sketch, preferred_...]
    unnamed x12 -> x16, local copies, waits for them, and re-layouts: 24.1 us -> 2.49 us
  transfers between devices with their start and end apart: 2 -> 15, of which waited for: 2 -> 7; matrix products, arithmetic and copies ran while one was open for 1% -> 13% of each run, Pallas kernels for 0% -> 3%
where the time goes in v1:
time: 373 us; the launch traced here: 372 us
  waiting for transfers between devices  206 us (55%)
  matrix products  50.6 us (14%)
  Pallas kernels  38.4 us (10%)
  local copies, waits for them, and re-layouts  20.9 us (6%)
  blocking collectives  19 us (5%)
  starting transfers between devices  16.3 us (4%)
  between operations  13.3 us (4%)
  other arithmetic  7.27 us (2%)
    all_gather x2, waiting for transfers between devices, shards(): sketches.append(lax.all_gather(own, 'rep', axis=0, tiled=True))  90.8 us
    all_gather x1, waiting for transfers between devices, shards(): lax.all_gather(mine.astype(jnp.bfloat16), 'rep', axis=0, tiled=False)  56.5 us
    ppermute x3, waiting for transfers between devices, hop(): return lax.ppermute(value, 'expert', [(p, p ^ bit) for p in range(experts)])  46.6 us
    dot_general x4, matrix products, project(): lax.dot_general(weight, sketch, (((0,), (0,)), ((), ())), preferred_eleme...  46 us
    pallas_call x2, Pallas kernels, gram(): pl.pallas_call(lambda *refs: gram_kernel(*refs, which=which, per=per, d=d...  21.5 us
    all_to_all x1, blocking collectives, shards(): own = lax.all_to_all(own, 'expert', split_axis=0, concat_axis=0, tiled=True)  16.4 us
    dynamic_update_slice x8, local copies, waits for them, and re-layouts, share(): result = lax.dynamic_update_slice(result, block[None, None], start)  12 us
    pallas_call x1, Pallas kernels, weave(): pl.pallas_call(weave_kernel, out_shape=jax.ShapeDtypeStruct((block, per,...  10.2 us
  transfers between devices with their start and end apart: 15, of which 7 were waited for; matrix products, arithmetic and copies ran while one was open for 13% of the time, Pallas kernels for 3%

profile of v1, /device:TPU:0, one launch (start us, length us, event | category | flops | bytes accessed | tf_op | source)
XLA Modules:
  0.0 371.6 jit_solution(10495272666022409674)
XLA Ops:
  7.4 2.7 multiply_reduce_fusion
  11.2 6.6 %flip.1 = bf16[16,208,512]{2,1,0:T(8,128)(2,1)} custom-call(bf16[512,3072]{1,0:T(8,128)(2,1)} %refs_0_.1, bf16[16,512]{1,0:T(8,128)(2,1)} %copy-done.4), custom_call_target="tpu_custom_call" | custom-call | flops 1572864 | bytes 6291456 | tf_op jit(solution)/shard_map/flip/pallas_call | solution.py:42
  17.8 8.4 %all-to-all-start = ((bf16[16,208,512]{2,1,0:T(8,128)(2,1)}), bf16[16,208,512]{2,1,0:T(8,128)(2,1)}, u32[]{:S(2)}, u32[]{:S(2)}) async-start(bf16[16,208,512]{2,1,0:T(8,128)(2,1)} %flip.1), calls=%async_computation | async-start | bytes 6815744 | tf_op jit(solution)/shard_map/all_to_all | solution.py:183
  26.3 4.6 %fusion.15 = f32[512,512]{1,0:T(8,128)S(1)} fusion(bf16[512,3072]{1,0:T(8,128)(2,1)S(1)} %copy-done, s32[3072,512]{1,0:T(8,128)} %param.10), kind=kOutput, calls=%fused_computation.14 | convolution fusion | flops 1612185600 | bytes 10485760 | tf_op jit(solution)/shard_map/dot_general | solution.py:184
  35.7 56.5 %all-gather.9.cloned.1.call-done = bf16[1024,512]{1,0:T(8,128)(2,1)} async-done(((bf16[256,512]{1,0:T(8,128)(2,1)}), bf16[1024,512]{1,0:T(8,128)(2,1)}) %all-gather.9.cloned.1.call-update) | async-done | bytes 1048592 | tf_op jit(solution)/shard_map/all_gather | solution.py:192
  92.2 3.0 collective-permute-start.4
  95.7 32.0 %collective-permute-done.2 = bf16[4,256,512]{2,1,0:T(8,128)(2,1)} collective-permute-done((bf16[4,256,512]{2,1,0:T(8,128)(2,1)}, bf16[4,256,512]{2,1,0:T(8,128)(2,1)}, u32[]{:S(2)}, u32[]{:S(2)}) %collective-permute-start.2) | collective-permute-done | bytes 1048608 | tf_op jit(solution)/shard_map/ppermute | solution.py:152
  129.4 4.3 %broadcast_in_dim.31 = bf16[4,2,4,256,512]{4,3,2,1,0:T(8,128)(2,1)} broadcast(bf16[]{:T(256)} %constant.84.clone.1), dimensions={} | broadcast | bytes 8388610 | tf_op jit(solution)/shard_map/broadcast_in_dim | solution.py:158
  135.3 14.6 %collective-permute-done.6 = bf16[4,256,512]{2,1,0:T(8,128)(2,1)S(1)} collective-permute-done((bf16[4,256,512]{2,1,0:T(8,128)(2,1)}, bf16[4,256,512]{2,1,0:T(8,128)(2,1)S(1)}, u32[]{:S(2)}, u32[]{:S(2)}) %collective-permute-start.6) | collective-permute-done | bytes 1048608 | tf_op jit(solution)/shard_map/ppermute | solution.py:152
  150.0 2.3 bitcast_dynamic-update-slice_fusion.6
  154.5 2.3 bitcast_dynamic-update-slice_fusion.4
  162.2 2.6 psum.7
  165.4 10.8 %gram.3 = bf16[4,192,512]{2,1,0:T(8,128)(2,1)} custom-call(f32[8]{0:T(128)} %copy-done.5, f32[8]{0:T(128)} %multiply_divide_fusion.refs_1_, bf16[16,208,512]{2,1,0:T(8,128)(2,1)} %all-to-all-done.refs_2_, bf16[4,2,4,256,512]{4,3,2,1,0:T(8,128)(2,1)} %bitcast_dynamic-update-slice_fusion.refs_3_, s32[192,512]{1,0:T(8,128)} %constant_dynamic-slice_fusion.refs_4_), custom_call_target="tpu_custom_call" | custom-call | flops 6442450944 | bytes 11796480 | tf_op jit(solution)/shard_map/gram/pallas_call | solution.py:93
  176.1 16.4 %all_to_all.15 = bf16[4,192,512]{2,1,0:T(8,128)(2,1)} all-to-all(bf16[4,192,512]{2,1,0:T(8,128)(2,1)} %gram.3), channel_id=1, replica_groups=mesh['expert'=4,'rep'=4,'hid'=2] {'expert'}, dimensions={0} | all-to-all | bytes 1572864 | tf_op jit(solution)/shard_map/all_to_all | solution.py:207
  192.5 10.8 %gram.2 = bf16[4,192,512]{2,1,0:T(8,128)(2,1)} custom-call(f32[8]{0:T(128)} %copy-done.5, f32[8]{0:T(128)} %multiply_divide_fusion.refs_1_, bf16[16,208,512]{2,1,0:T(8,128)(2,1)} %all-to-all-done.refs_2_, bf16[4,2,4,256,512]{4,3,2,1,0:T(8,128)(2,1)} %bitcast_dynamic-update-slice_fusion.refs_3_, s32[192,512]{1,0:T(8,128)} %constant_dynamic-slice_fusion.refs_4_), custom_call_target="tpu_custom_call" | custom-call | flops 6442450944 | bytes 11796480 | tf_op jit(solution)/shard_map/gram/pallas_call | solution.py:93
  203.3 3.5 all-to-all-start.1
  207.0 10.0 %all-to-all-done.1 = bf16[4,192,512]{2,1,0:T(8,128)(2,1)S(1)} async-done(((bf16[4,192,512]{2,1,0:T(8,128)(2,1)}), bf16[4,192,512]{2,1,0:T(8,128)(2,1)S(1)}, u32[]{:S(2)}, u32[]{:S(2)}) %all-to-all-start.1) | async-done | bytes 786464 | tf_op jit(solution)/shard_map/all_to_all | solution.py:207
  218.0 40.6 %all-gather.7.cloned.1.call-done = bf16[3072,512]{1,0:T(8,128)(2,1)} async-done(((bf16[768,512]{1,0:T(8,128)(2,1)}), bf16[3072,512]{1,0:T(8,128)(2,1)}) %all-gather.7.cloned.1.call-update) | async-done | bytes 3145744 | tf_op jit(solution)/shard_map/all_gather | solution.py:211
  258.6 13.5 %fusion.4 = f32[2048,512]{1,0:T(8,128)} fusion(bf16[3072,512]{1,0:T(8,128)(2,1)} %all-gather.7.cloned.1.call-done, bf16[2,3072,4096]{2,1,0:T(8,128)(2,1)} %param.11, s32[]{:T(128)S(6)} %select_n.55), kind=kOutput, calls=%fused_computation.4 | convolution fusion | flops 6442450944 | bytes 19922948 | tf_op jit(solution)/shard_map/dot_general | solution.py:217
  272.1 50.2 %all-gather.5.cloned.1.call-done = bf16[3072,512]{1,0:T(8,128)(2,1)} async-done(((bf16[768,512]{1,0:T(8,128)(2,1)}), bf16[3072,512]{1,0:T(8,128)(2,1)}) %all-gather.5.cloned.1.call-update) | async-done | bytes 3145744 | tf_op jit(solution)/shard_map/all_gather | solution.py:211
  322.3 11.8 %fusion.12.refs_0_ = f32[2048,512]{1,0:T(8,128)} fusion(f32[2048,512]{1,0:T(8,128)} %collective-permute-done.8, bf16[3072,512]{1,0:T(8,128)(2,1)S(1)} %copy-done.6, bf16[2,3072,4096]{2,1,0:T(8,128)(2,1)} %param.11, s32[]{:T(128)S(6)} %select_n.54), kind=kOutput, calls=%fused_computation.13 | convolution fusion | flops 6443499520 | bytes 24117252 | tf_op jit(solution)/shard_map/dot_general | solution.py:217
  334.1 9.7 %fusion = f32[2048,512]{1,0:T(8,128)S(1)} fusion(bf16[3072,512]{1,0:T(8,128)(2,1)S(1)} %copy-done.7, bf16[2,3072,4096]{2,1,0:T(8,128)(2,1)} %param.11, s32[]{:T(128)S(6)} %select_n.55), kind=kOutput, calls=%fused_computation | convolution fusion | flops 6442450944 | bytes 19922948 | tf_op jit(solution)/shard_map/dot_general | solution.py:217
  343.9 11.0 %fusion.2.refs_1_ = f32[2048,512]{1,0:T(8,128)} fusion(bf16[3072,512]{1,0:T(8,128)(2,1)S(1)} %copy-done.7, bf16[2,3072,4096]{2,1,0:T(8,128)(2,1)} %param.11, s32[]{:T(128)S(6)} %select_n.54), kind=kOutput, calls=%fused_computation.2 | convolution fusion | flops 6442450944 | bytes 19922948 | tf_op jit(solution)/shard_map/dot_general | solution.py:217
  354.9 10.2 %weave.1 = f32[2048,2,512]{2,1,0:T(2,128)} custom-call(f32[2048,512]{1,0:T(8,128)} %fusion.12.refs_0_, f32[2048,512]{1,0:T(8,128)} %fusion.2.refs_1_, f32[2048,512]{1,0:T(8,128)} %collective-permute-done.9.refs_2_), custom_call_target="tpu_custom_call" | custom-call | flops 1048576 | bytes 20971520 | tf_op jit(solution)/shard_map/weave/pallas_call | solution.py:131
  (59 shorter events, 20.0 us)
Async XLA Ops:
  6.5 19.7 %copy-start = (bf16[512,3072]{1,0:T(8,128)(2,1)S(1)}, bf16[512,3072]{1,0:T(8,128)(2,1)}, u32[]{:S(2)}) copy-start(bf16[512,3072]{1,0:T(8,128)(2,1)} %refs_0_.1) | copy-start | bytes 9437188
  10.5 0.6 copy-start.4
  17.8 143.1 %all-to-all-start = ((bf16[16,208,512]{2,1,0:T(8,128)(2,1)}), bf16[16,208,512]{2,1,0:T(8,128)(2,1)}, u32[]{:S(2)}, u32[]{:S(2)}) async-start(bf16[16,208,512]{2,1,0:T(8,128)(2,1)} %flip.1), calls=%async_computation | async-start | bytes 6815744 | tf_op jit(solution)/shard_map/all_to_all | solution.py:183
  26.2 66.0 %all-gather.9.cloned.1.call-start = ((), (), s32[]{:S(2)}) async-start(), calls=%async_computation.5 | async-start | bytes 1310720 | tf_op jit(solution)/shard_map/all_gather | solution.py:192
  30.8 1.0 copy-start.2
  31.9 2.0 collective-permute-start
  35.7 222.9 %all-gather.7.cloned.1.call-start = ((), (), s32[]{:S(2)}) async-start(), calls=%async_computation.4 | async-start | bytes 3932160 | tf_op jit(solution)/shard_map/all_gather | solution.py:211
  92.2 41.6 %copy-start.3 = (bf16[1024,512]{1,0:T(8,128)(2,1)S(1)}, bf16[1024,512]{1,0:T(8,128)(2,1)}, u32[]{:S(2)}) copy-start(bf16[1024,512]{1,0:T(8,128)(2,1)} %all-gather.9.cloned.1.call-done) | copy-start | bytes 3145732
  92.2 35.5 %collective-permute-start.2 = (bf16[4,256,512]{2,1,0:T(8,128)(2,1)}, bf16[4,256,512]{2,1,0:T(8,128)(2,1)}, u32[]{:S(2)}, u32[]{:S(2)}) collective-permute-start(bf16[4,256,512]{2,1,0:T(8,128)(2,1)} %bitcast.53), channel_id=1, source_target_pairs={{0,8},{8,0},{16,24},{24,16},{1,9},{9,1},{17,25},{25,17},{2,10},{10... | collective-permute-start | bytes 3145736 | tf_op jit(solution)/shard_map/ppermute | solution.py:152
  92.2 42.6 %collective-permute-start.4 = (bf16[4,256,512]{2,1,0:T(8,128)(2,1)}, bf16[4,256,512]{2,1,0:T(8,128)(2,1)S(1)}, u32[]{:S(2)}, u32[]{:S(2)}) collective-permute-start(bf16[4,256,512]{2,1,0:T(8,128)(2,1)} %bitcast.54), channel_id=1, source_target_pairs={{0,16},{8,24},{16,0},{24,8},{1,17},{9,25},{17,1},{25,9},{2,18},{10... | collective-permute-start | bytes 3145736 | tf_op jit(solution)/shard_map/ppermute | solution.py:152
  95.2 54.7 %collective-permute-start.6 = (bf16[4,256,512]{2,1,0:T(8,128)(2,1)}, bf16[4,256,512]{2,1,0:T(8,128)(2,1)S(1)}, u32[]{:S(2)}, u32[]{:S(2)}) collective-permute-start(bf16[4,256,512]{2,1,0:T(8,128)(2,1)} %bitcast.55), channel_id=1, source_target_pairs={{0,24},{8,16},{16,8},{24,0},{1,25},{9,17},{17,9},{25,1},{2,26},{10... | collective-permute-start | bytes 3145736 | tf_op jit(solution)/shard_map/ppermute | solution.py:152
  95.7 54.3 %collective-permute-start.1 = (bf16[4,256,512]{2,1,0:T(8,128)(2,1)}, bf16[4,256,512]{2,1,0:T(8,128)(2,1)}, u32[]{:S(2)}, u32[]{:S(2)}) collective-permute-start(bf16[4,256,512]{2,1,0:T(8,128)(2,1)} %bitcast.56), channel_id=1, source_target_pairs={{0,1},{1,0},{2,3},{3,2},{4,5},{5,4},{6,7},{7,6},{8,9},{9,8},{10,11... | collective-permute-start | bytes 3145736 | tf_op jit(solution)/shard_map/ppermute | solution.py:155
  127.7 26.8 %collective-permute-start.3 = (bf16[4,256,512]{2,1,0:T(8,128)(2,1)}, bf16[4,256,512]{2,1,0:T(8,128)(2,1)}, u32[]{:S(2)}, u32[]{:S(2)}) collective-permute-start(bf16[4,256,512]{2,1,0:T(8,128)(2,1)} %collective-permute-done.2), channel_id=1, source_target_pairs={{0,1},{1,0},{2,3},{3,2},{4,5},{5,4},{6,7},{7,6},{8,9},{9,8},{10,11... | collective-permute-start | bytes 3145736 | tf_op jit(solution)/shard_map/ppermute | solution.py:155
  134.8 23.0 %collective-permute-start.5 = (bf16[4,256,512]{2,1,0:T(8,128)(2,1)S(1)}, bf16[4,256,512]{2,1,0:T(8,128)(2,1)S(1)}, u32[]{:S(2)}, u32[]{:S(2)}) collective-permute-start(bf16[4,256,512]{2,1,0:T(8,128)(2,1)S(1)} %collective-permute-done.4), channel_id=1, source_target_pairs={{0,1},{1,0},{2,3},{3,2},{4,5},{5,4},{6,7},{7,6},{8,9},{9,8},{10,11... | collective-permute-start | bytes 3145736 | tf_op jit(solution)/shard_map/ppermute | solution.py:155
  150.0 9.9 %collective-permute-start.7 = (bf16[4,256,512]{2,1,0:T(8,128)(2,1)S(1)}, bf16[4,256,512]{2,1,0:T(8,128)(2,1)S(1)}, u32[]{:S(2)}, u32[]{:S(2)}) collective-permute-start(bf16[4,256,512]{2,1,0:T(8,128)(2,1)S(1)} %collective-permute-done.6), channel_id=1, source_target_pairs={{0,1},{1,0},{2,3},{3,2},{4,5},{5,4},{6,7},{7,6},{8,9},{9,8},{10,11... | collective-permute-start | bytes 3145736 | tf_op jit(solution)/shard_map/ppermute | solution.py:155
  162.2 3.2 copy-start.5
  203.3 13.8 %all-to-all-start.1 = ((bf16[4,192,512]{2,1,0:T(8,128)(2,1)}), bf16[4,192,512]{2,1,0:T(8,128)(2,1)S(1)}, u32[]{:S(2)}, u32[]{:S(2)}) async-start(bf16[4,192,512]{2,1,0:T(8,128)(2,1)} %gram.2), calls=%async_computation.1 | async-start | bytes 1572864 | tf_op jit(solution)/shard_map/all_to_all | solution.py:207
  206.8 115.5 %all-gather.5.cloned.1.call-start = ((), (), s32[]{:S(2)}) async-start(), calls=%async_computation.3 | async-start | bytes 3932160 | tf_op jit(solution)/shard_map/all_gather | solution.py:211
  217.0 0.9 copy-start.1
  258.6 63.7 %copy-start.6 = (bf16[3072,512]{1,0:T(8,128)(2,1)S(1)}, bf16[3072,512]{1,0:T(8,128)(2,1)}, u32[]{:S(2)}) copy-start(bf16[3072,512]{1,0:T(8,128)(2,1)} %all-gather.7.cloned.1.call-done) | copy-start | bytes 9437188
  272.1 50.2 %collective-permute-start.8 = (f32[2048,512]{1,0:T(8,128)}, f32[2048,512]{1,0:T(8,128)}, u32[]{:S(2)}, u32[]{:S(2)}) collective-permute-start(f32[2048,512]{1,0:T(8,128)} %fusion.4), channel_id=1, source_target_pairs={{0,1},{1,0},{2,3},{3,2},{4,5},{5,4},{6,7},{7,6},{8,9},{9,8},{10,11... | collective-permute-start | bytes 12582920 | tf_op jit(solution)/shard_map/ppermute | solution.py:228
  322.3 11.8 %copy-start.7 = (bf16[3072,512]{1,0:T(8,128)(2,1)S(1)}, bf16[3072,512]{1,0:T(8,128)(2,1)}, u32[]{:S(2)}) copy-start(bf16[3072,512]{1,0:T(8,128)(2,1)} %all-gather.5.cloned.1.call-done) | copy-start | bytes 9437188
  343.8 11.1 %collective-permute-start.9 = (f32[2048,512]{1,0:T(8,128)S(1)}, f32[2048,512]{1,0:T(8,128)}, u32[]{:S(2)}, u32[]{:S(2)}) collective-permute-start(f32[2048,512]{1,0:T(8,128)S(1)} %fusion), channel_id=1, source_target_pairs={{0,1},{1,0},{2,3},{3,2},{4,5},{5,4},{6,7},{7,6},{8,9},{9,8},{10,11... | collective-permute-start | bytes 12582920 | tf_op jit(solution)/shard_map/ppermute | solution.py:228
Sparse Core Ops, SparseCore 0:
  35.8 56.3 all-gather.8
  192.6 65.9 all-gather.6
  260.2 62.0 all-gather.4

commit v2 on v1

--- a/solution.py
+++ b/solution.py
@@ -55,7 +55,8 @@
     )(calib_rows, extra)
 
 
-def gram_kernel(counts_ref, ridge_ref, x_ref, m_ref, s_ref, o_ref, lhs, acc, *, which, per, d):
+def gram_kernel(counts_ref, ridge_ref, at_ref, x_ref, s_ref, *rest, which, per, d):
+    m_refs, (o_ref, lhs, acc, right) = rest[:-4], rest[-4:]
     step = pl.program_id(0)
     groups = o_ref.shape[0]
     sources, _, tokens = x_ref.shape
@@ -65,8 +66,16 @@
             row = d + g * per + which
             lhs[g, :, s * tokens : (s + 1) * tokens] = x * x_ref[s, row : row + 1, :]
     flat = lhs[...].reshape(groups * d, sources * tokens)
-    rows = m_ref[...].reshape(sources * tokens, m_ref.shape[-1])
-    part = jnp.dot(flat, rows, preferred_element_type=jnp.float32)
+    if len(m_refs) == 1:
+        right[...] = m_refs[0][...].reshape(right.shape)
+    else:
+        me, h = at_ref[0], at_ref[1]
+        half = tokens // 2
+        for i, m_ref in enumerate(m_refs):
+            side = h if i % 2 == 0 else 1 - h
+            row = pl.multiple_of(((me ^ (i // 2)) * 2 + side) * half, half)
+            right[pl.ds(row, half), :] = m_ref[0]
+    part = jnp.dot(flat, right[...], preferred_element_type=jnp.float32)
 
     @pl.when(step == 0)
     def _():
@@ -85,10 +94,17 @@
             o_ref[g] = (total / counts_ref[e] + ridge_ref[e] * signs).astype(jnp.bfloat16)
 
 
-def gram(counts, ridge, received, sketched, signs, which, per):
+def gram(counts, ridge, at, received, sketched, signs, which, per):
     sources, rows, tokens = received.shape
     d = rows - EXTRA
-    batch, hid, _, share, width = sketched.shape
+    width = signs.shape[1]
+    if isinstance(sketched, list):
+        batch = len(sketched) // 2
+        m_specs = [pl.BlockSpec((1, tokens // 2, width), lambda j: (j, 0, 0))] * len(sketched)
+    else:
+        batch, hid, _, part = sketched.shape[:4]
+        m_specs = [pl.BlockSpec((batch, hid, 1, part, width), lambda j: (0, 0, j, 0, 0))]
+        sketched = [sketched]
     groups = EXPERTS // per
     return pl.pallas_call(
         lambda *refs: gram_kernel(*refs, which=which, per=per, d=d),
@@ -97,14 +113,16 @@
         in_specs=[
             pl.BlockSpec(memory_space=pltpu.SMEM),
             pl.BlockSpec(memory_space=pltpu.SMEM),
+            pl.BlockSpec(memory_space=pltpu.SMEM),
             pl.BlockSpec((batch, rows, tokens), lambda j: (j, 0, 0)),
-            pl.BlockSpec((batch, hid, 1, share, width), lambda j: (0, 0, j, 0, 0)),
             pl.BlockSpec((d, width), lambda j: (0, 0)),
+            *m_specs,
         ],
         out_specs=pl.BlockSpec((groups, d, width), lambda j: (0, 0, 0)),
         scratch_shapes=[
             pltpu.VMEM((groups, d, batch * tokens), jnp.bfloat16),
             pltpu.VMEM((groups * d, width), jnp.float32),
+            pltpu.VMEM((batch * tokens, width), jnp.bfloat16),
         ],
         cost_estimate=pl.CostEstimate(
             flops=2 * sources * groups * d * tokens * width,
@@ -112,24 +130,23 @@
             transcendentals=0,
         ),
         name="gram",
-    )(counts, ridge, received, sketched, signs)
-
-
-def weave_kernel(*refs):
-    fresh_ref, away_ref, o_ref = refs[-3], refs[-2], refs[-1]
-    done = refs[:-3]
-    for k, ref in enumerate(done):
-        o_ref[:, k, :] = ref[...]
-    o_ref[:, len(done), :] = fresh_ref[...] + away_ref[...]
-
-
-def weave(done, fresh, away):
-    block, width = fresh.shape
-    per = len(done) + 1
+    )(counts, ridge, at, received, signs, *sketched)
+
+
+def weave_kernel(*refs, fresh):
+    away_ref, o_ref = refs[-2:]
+    for k, ref in enumerate(refs[:-2]):
+        value = ref[...]
+        o_ref[:, k, :] = value + away_ref[...] if k == fresh else value
+
+
+def weave(parts, fresh, away):
+    block, width = away.shape
+    per = len(parts)
     tile = math.gcd(block, 256)
     spec = pl.BlockSpec((tile, width), lambda i: (i, 0))
     return pl.pallas_call(
-        weave_kernel,
+        lambda *refs: weave_kernel(*refs, fresh=fresh),
         out_shape=jax.ShapeDtypeStruct((block, per, width), jnp.float32),
         grid=(block // tile,),
         in_specs=[spec] * (per + 1),
@@ -138,7 +155,7 @@
             flops=block * width, bytes_accessed=4 * block * width * (2 * per + 1), transcendentals=0
         ),
         name="weave",
-    )(*done, fresh, away)
+    )(*parts, away)
 
 
 def share(rows):
@@ -146,7 +163,6 @@
     if experts != 4 or hid != 2:
         rows = lax.all_gather(rows, ("expert", "hid"), axis=0, tiled=False)
         return rows.reshape(experts, hid, *rows.shape[1:])
-    me, h = lax.axis_index("expert"), lax.axis_index("hid")
 
     def hop(value, bit):
         return lax.ppermute(value, "expert", [(p, p ^ bit) for p in range(experts)])
@@ -154,13 +170,35 @@
     def across(value):
         return lax.ppermute(value, "hid", [(0, 1), (1, 0)])
 
-    parts = [rows] + [hop(rows, bit) for bit in range(1, experts)]
-    result = jnp.zeros((experts, hid, *rows.shape), rows.dtype)
-    for bit, value in enumerate(parts):
-        for side, block in ((h, value), (1 - h, across(value))):
-            start = (me ^ bit, side) + (0,) * rows.ndim
-            result = lax.dynamic_update_slice(result, block[None, None], start)
-    return result
+    half = rows.shape[0] // 2
+    one, two = hop(rows, 1), hop(rows, 2)
+    both = [hop(two[:half], 1), hop(one[half:], 2)]
+    both = jnp.concatenate(both, axis=0)
+    blocks = []
+    for value in (rows, one, two, both):
+        blocks += [value, across(value)]
+    return blocks
+
+
+def ring(own, others):
+    size, me = lax.axis_size("rep"), lax.axis_index("rep")
+    right, left, ups, downs = own, own, [], []
+    for step in range(1, size):
+        ups_pairs = [(p, p + 1) for p in range(step - 1, size - 1)]
+        down_pairs = [(p + 1, p) for p in range(size - step)]
+        right = lax.ppermute(right, "rep", ups_pairs)
+        left = lax.ppermute(left, "rep", down_pairs)
+        if step == 1:
+            right, left = lax.optimization_barrier((right, left, others))[:2]
+        ups.append(right)
+        downs.append(left)
+    result = jnp.zeros((size, *own.shape), own.dtype)
+    result = lax.dynamic_update_slice(result, own[None], (me, 0, 0))
+    for step in range(1, size):
+        block = jnp.where(me >= step, ups[step - 1], downs[size - 1 - step])
+        start = ((me - step) % size, 0, 0)
+        result = lax.dynamic_update_slice(result, block[None], start)
+    return result.reshape(size * own.shape[0], own.shape[1])
 
 
 def shards(calib_rows, routes, sketch_seed, up_weight):
@@ -197,19 +235,24 @@
     square_sums = lax.psum(jnp.sum(stats[:, EXPERTS : EXPERTS + 3, :EXPERTS], axis=(0, 1)), "hid")
     ridge = damping * square_sums / (counts * D)
     place = lax.axis_index(("rep", "expert"))
+    at = jnp.stack([lax.axis_index("expert"), h]).astype(jnp.int32)
     signs = lax.dynamic_slice_in_dim(sketch_seed, place * d, d, 0)
 
     block = full // hid
     swap = [(0, 1), (1, 0)]
-    outs, owns = [], []
+    owns = []
     for k in range(per):
-        own = gram(counts, ridge, received, sketched, signs, k, per)
+        own = gram(counts, ridge, at, received, sketched, signs, k, per)
         own = lax.all_to_all(own, "expert", split_axis=0, concat_axis=0, tiled=True)
         owns.append(own.reshape(-1, width))
     sketches = []
     for k, own in enumerate(owns):
-        sketches.append(lax.all_gather(own, "rep", axis=0, tiled=True))
-    for k in range(per):
+        if hid == 2 and k == per - 1:
+            sketches.append(ring(own, owns[:k]))
+        else:
+            sketches.append(lax.all_gather(own, "rep", axis=0, tiled=True))
+    outs = [None] * per
+    for turn, k in enumerate(reversed(range(per))):
         sketch = lax.optimization_barrier((sketches[k], owns))[0]
 
         def project(start, size):
@@ -219,16 +262,15 @@
             )
 
         if hid != 2:
-            outs.append(
-                lax.psum_scatter(project(0, full), "hid", scatter_dimension=0, tiled=True)
-            )
+            outs[k] = lax.psum_scatter(project(0, full), "hid", scatter_dimension=0, tiled=True)
             continue
-        if outs:
-            sketch, outs = lax.optimization_barrier((sketch, outs))
+        if turn:
+            sketch, outs[k + 1] = lax.optimization_barrier((sketch, outs[k + 1]))
         away = lax.ppermute(project((1 - h) * block, block), "hid", swap)
-        if k == per - 1:
-            return weave(outs, project(h * block, block), away)
-        outs.append(project(h * block, block) + away)
+        if turn == per - 1:
+            outs[k] = project(h * block, block)
+            return weave(outs, k, away)
+        outs[k] = project(h * block, block) + away
     return jnp.stack(outs, axis=1)
 
 

time: 373 us -> 354 us (0.949)
  waiting for transfers between devices: 206 us -> 173 us
  local copies, waits for them, and re-layouts: 20.9 us -> 5.72 us
  blocking collectives: 19 us -> 32.6 us
  starting transfers between devices: 16.3 us -> 26.2 us
    all_gather x2 -> x1, waiting for transfers between devices: 90.8 us -> 24.2 us  [shards(): sketches.append(lax.all_gather(own, 'rep', axis=0, tiled=True))]
    ppermute x0 -> x6, waiting for transfers between devices: none -> 48.2 us  [the longest x3 48.2 us: ring(): left = lax.ppermute(left, 'rep', down_pairs)]
    all_to_all x1 -> x2, blocking collectives: 16.4 us -> 30 us  [shards(): own = lax.all_to_all(own, 'expert', split_axis=0, concat_axis=0, tiled=True)]
    dynamic_update_slice x8 -> x1, local copies, waits for them, and re-layouts: 12 us -> 0.06 us  [ring(): result = lax.dynamic_update_slice(result, own[None], (me, 0, 0))]
    ppermute x0 -> x6, starting transfers between devices: none -> 11.6 us  [the longest x3 7.75 us: ring(): right = lax.ppermute(right, 'rep', ups_pairs)]
    all_to_all x1 -> x0, waiting for transfers between devices: 10 us -> none  [shards(): own = lax.all_to_all(own, 'expert', split_axis=0, concat_axis=0, tiled=True)]
    ppermute x3 -> x4, waiting for transfers between devices: 46.6 us -> 41.9 us  [hop(): return lax.ppermute(value, 'expert', [(p, p ^ bit) for p in range(experts)])]
    broadcast_in_dim x1, local copies, waits for them, and re-layouts: 4.34 us -> 0.24 us  [ring(): result = jnp.zeros((size, *own.shape), own.dtype)]
  transfers between devices with their start and end apart: 15 -> 20, of which waited for: 7 -> 8; matrix products, arithmetic and copies ran while one was open for 13% -> 11% of each run, Pallas kernels for 3% -> 3%
where the time goes in v2:
time: 354 us; the launch traced here: 353 us
  waiting for transfers between devices  173 us (49%)
  matrix products  52.4 us (15%)
  Pallas kernels  40.4 us (11%)
  blocking collectives  32.6 us (9%)
  starting transfers between devices  26.2 us (7%)
  between operations  13.7 us (4%)
  other arithmetic  9.39 us (3%)
  local copies, waits for them, and re-layouts  5.72 us (2%)
    all_gather x1, waiting for transfers between devices, shards(): lax.all_gather(mine.astype(jnp.bfloat16), 'rep', axis=0, tiled=False)  56.5 us
    ppermute x3, waiting for transfers between devices, ring(): left = lax.ppermute(left, 'rep', down_pairs)  48.2 us
    dot_general x4, matrix products, project(): lax.dot_general(weight, sketch, (((0,), (0,)), ((), ())), preferred_eleme...  47.8 us
    ppermute x4, waiting for transfers between devices, hop(): return lax.ppermute(value, 'expert', [(p, p ^ bit) for p in range(experts)])  41.9 us
    all_to_all x2, blocking collectives, shards(): own = lax.all_to_all(own, 'expert', split_axis=0, concat_axis=0, tiled=True)  30 us
    all_gather x1, waiting for transfers between devices, shards(): sketches.append(lax.all_gather(own, 'rep', axis=0, tiled=True))  24.2 us
    pallas_call x2, Pallas kernels, gram(): pl.pallas_call(lambda *refs: gram_kernel(*refs, which=which, per=per, d=d...  23.6 us
    pallas_call x1, Pallas kernels, weave(): pl.pallas_call(lambda *refs: weave_kernel(*refs, fresh=fresh), out_shape=...  10.2 us
  transfers between devices with their start and end apart: 20, of which 8 were waited for; matrix products, arithmetic and copies ran while one was open for 11% of the time, Pallas kernels for 3%

profile of v2, /device:TPU:0, one launch (start us, length us, event | category | flops | bytes accessed | tf_op | source)
XLA Modules:
  0.0 353.1 jit_solution(17263347204262230623)
XLA Ops:
  6.5 2.6 multiply_reduce_fusion
  10.9 6.6 %flip.1 = bf16[16,208,512]{2,1,0:T(8,128)(2,1)} custom-call(bf16[512,3072]{1,0:T(8,128)(2,1)} %refs_0_.1, bf16[16,512]{1,0:T(8,128)(2,1)} %copy-done.5), custom_call_target="tpu_custom_call" | custom-call | flops 1572864 | bytes 6291456 | tf_op jit(solution)/shard_map/flip/pallas_call | solution.py:42
  17.5 8.6 %all-to-all-start = ((bf16[16,208,512]{2,1,0:T(8,128)(2,1)}), bf16[16,208,512]{2,1,0:T(8,128)(2,1)}, u32[]{:S(2)}, u32[]{:S(2)}) async-start(bf16[16,208,512]{2,1,0:T(8,128)(2,1)} %flip.1), calls=%async_computation | async-start | bytes 6815744 | tf_op jit(solution)/shard_map/all_to_all | solution.py:221
  26.2 4.6 %fusion.15 = f32[512,512]{1,0:T(8,128)S(1)} fusion(bf16[512,3072]{1,0:T(8,128)(2,1)S(1)} %copy-done, s32[3072,512]{1,0:T(8,128)} %param.10), kind=kOutput, calls=%fused_computation.14 | convolution fusion | flops 1612185600 | bytes 10485760 | tf_op jit(solution)/shard_map/dot_general | solution.py:222
  31.9 1.9 collective-permute-done
  33.8 1.8 add_convert_fusion
  35.7 56.5 %all-gather.6.cloned.1.call-done = bf16[1024,512]{1,0:T(8,128)(2,1)} async-done(((bf16[256,512]{1,0:T(8,128)(2,1)}), bf16[1024,512]{1,0:T(8,128)(2,1)}) %all-gather.6.cloned.1.call-update) | async-done | bytes 1048592 | tf_op jit(solution)/shard_map/all_gather | solution.py:230
  95.2 31.0 %collective-permute-done.4.refs_9_ = bf16[4,256,512]{2,1,0:T(8,128)(2,1)S(1)} collective-permute-done((bf16[4,256,512]{2,1,0:T(8,128)(2,1)}, bf16[4,256,512]{2,1,0:T(8,128)(2,1)S(1)}, u32[]{:S(2)}, u32[]{:S(2)}) %collective-permute-start.4) | collective-permute-done | bytes 1048608 | tf_op jit(solution)/shard_map/ppermute | solution.py:168
  129.0 10.2 %collective-permute-done.6 = bf16[2,256,512]{2,1,0:T(8,128)(2,1)S(1)} collective-permute-done((bf16[2,256,512]{2,1,0:T(8,128)(2,1)S(1)}, bf16[2,256,512]{2,1,0:T(8,128)(2,1)S(1)}, u32[]{:S(2)}, u32[]{:S(2)}) %collective-permute-start.6) | collective-permute-done | bytes 524320 | tf_op jit(solution)/shard_map/ppermute | solution.py:168
  141.6 1.8 constant_dynamic-slice_fusion.1.refs_4_
  144.9 2.6 psum.7
  148.3 11.8 %gram.3 = bf16[4,192,512]{2,1,0:T(8,128)(2,1)} custom-call(f32[8]{0:T(128)} %copy-done.6, f32[8]{0:T(128)} %multiply_divide_fusion.refs_1_, s32[2]{0:T(128)} %pad_add_fusion.refs_2_, bf16[16,208,512]{2,1,0:T(8,128)(2,1)} %all-to-all-done.refs_3_, s32[192,512]{1,0:T(8,128)} %constant_dynamic-slice_fusion.1.refs_4_, bf16[4,256,512]{2,1,0:T(8,128)(2,1)} %bitcast.58, ...), custom_call_target="tpu_custom_call" | custom-call | flops 6442450944 | bytes 11796480 | tf_op jit(solution)/shard_map/gram/pallas_call | solution.py:109
  160.1 15.6 %all_to_all.15 = bf16[4,192,512]{2,1,0:T(8,128)(2,1)S(1)} all-to-all(bf16[4,192,512]{2,1,0:T(8,128)(2,1)} %gram.3), channel_id=1, replica_groups=mesh['expert'=4,'rep'=4,'hid'=2] {'expert'}, dimensions={0} | all-to-all | bytes 1572864 | tf_op jit(solution)/shard_map/all_to_all | solution.py:246
  176.9 4.6 %collective-permute-start.9 = (bf16[768,512]{1,0:T(8,128)(2,1)S(1)}, bf16[768,512]{1,0:T(8,128)(2,1)S(1)}, u32[]{:S(2)}, u32[]{:S(2)}) collective-permute-start(bf16[768,512]{1,0:T(8,128)(2,1)S(1)} %bitcast.50), channel_id=1, source_target_pairs={{0,2},{2,4},{4,6},{1,3},{3,5},{5,7},{8,10},{10,12},{12,14},{9,11},... | collective-permute-start | bytes 2359304 | tf_op jit(solution)/shard_map/ppermute | solution.py:189
  181.5 11.8 %gram.2 = bf16[4,192,512]{2,1,0:T(8,128)(2,1)} custom-call(f32[8]{0:T(128)} %copy-done.6, f32[8]{0:T(128)} %multiply_divide_fusion.refs_1_, s32[2]{0:T(128)} %pad_add_fusion.refs_2_, bf16[16,208,512]{2,1,0:T(8,128)(2,1)} %all-to-all-done.refs_3_, s32[192,512]{1,0:T(8,128)} %constant_dynamic-slice_fusion.1.refs_4_, bf16[4,256,512]{2,1,0:T(8,128)(2,1)} %bitcast.59, ...), custom_call_target="tpu_custom_call" | custom-call | flops 6442450944 | bytes 11796480 | tf_op jit(solution)/shard_map/gram/pallas_call | solution.py:109
  193.3 14.5 %all_to_all.16 = bf16[4,192,512]{2,1,0:T(8,128)(2,1)} all-to-all(bf16[4,192,512]{2,1,0:T(8,128)(2,1)} %gram.2), channel_id=1, replica_groups=mesh['expert'=4,'rep'=4,'hid'=2] {'expert'}, dimensions={0} | all-to-all | bytes 1572864 | tf_op jit(solution)/shard_map/all_to_all | solution.py:246
  210.7 20.5 %collective-permute-done.11 = bf16[768,512]{1,0:T(8,128)(2,1)S(1)} collective-permute-done((bf16[768,512]{1,0:T(8,128)(2,1)S(1)}, bf16[768,512]{1,0:T(8,128)(2,1)S(1)}, u32[]{:S(2)}, u32[]{:S(2)}) %collective-permute-start.11) | collective-permute-done | bytes 786464 | tf_op jit(solution)/shard_map/ppermute | solution.py:190
  234.4 27.6 %collective-permute-done.12 = bf16[768,512]{1,0:T(8,128)(2,1)} collective-permute-done((bf16[768,512]{1,0:T(8,128)(2,1)S(1)}, bf16[768,512]{1,0:T(8,128)(2,1)}, u32[]{:S(2)}, u32[]{:S(2)}) %collective-permute-start.12) | collective-permute-done | bytes 786464 | tf_op jit(solution)/shard_map/ppermute | solution.py:190
  264.0 12.2 %fusion.2 = f32[2048,512]{1,0:T(8,128)} fusion(bf16[3072,512]{1,0:T(8,128)(2,1)S(1)} %bitcast.52, bf16[2,3072,4096]{2,1,0:T(8,128)(2,1)} %param.11, s32[]{:T(128)S(6)} %select_n.81), kind=kOutput, calls=%fused_computation.2 | convolution fusion | flops 6442450944 | bytes 19922948 | tf_op jit(solution)/shard_map/dot_general | solution.py:260
  276.2 24.2 %all-gather.4.cloned.1.call-done = bf16[3072,512]{1,0:T(8,128)(2,1)} async-done(((bf16[768,512]{1,0:T(8,128)(2,1)}), bf16[3072,512]{1,0:T(8,128)(2,1)}) %all-gather.4.cloned.1.call-update) | async-done | bytes 3145744 | tf_op jit(solution)/shard_map/all_gather | solution.py:253
  300.4 14.9 %fusion.12.refs_1_ = f32[2048,512]{1,0:T(8,128)} fusion(f32[2048,512]{1,0:T(8,128)} %collective-permute-done.15, bf16[3072,512]{1,0:T(8,128)(2,1)} %bitcast.53, bf16[2,3072,4096]{2,1,0:T(8,128)(2,1)} %param.11, s32[]{:T(128)S(6)} %select_n.64), kind=kOutput, calls=%fused_computation.13 | convolution fusion | flops 6443499520 | bytes 24117252 | tf_op jit(solution)/shard_map/dot_general | solution.py:260
  315.3 9.7 %fusion = f32[2048,512]{1,0:T(8,128)S(1)} fusion(bf16[3072,512]{1,0:T(8,128)(2,1)S(1)} %copy-done.7, bf16[2,3072,4096]{2,1,0:T(8,128)(2,1)} %param.11, s32[]{:T(128)S(6)} %select_n.81), kind=kOutput, calls=%fused_computation | convolution fusion | flops 6442450944 | bytes 19922948 | tf_op jit(solution)/shard_map/dot_general | solution.py:260
  325.1 11.0 %fusion.6.refs_0_ = f32[2048,512]{1,0:T(8,128)} fusion(bf16[3072,512]{1,0:T(8,128)(2,1)S(1)} %copy-done.7, bf16[2,3072,4096]{2,1,0:T(8,128)(2,1)} %param.11, s32[]{:T(128)S(6)} %select_n.64), kind=kOutput, calls=%fused_computation.6 | convolution fusion | flops 6442450944 | bytes 19922948 | tf_op jit(solution)/shard_map/dot_general | solution.py:260
  336.1 10.2 %weave.1 = f32[2048,2,512]{2,1,0:T(2,128)} custom-call(f32[2048,512]{1,0:T(8,128)} %fusion.6.refs_0_, f32[2048,512]{1,0:T(8,128)} %fusion.12.refs_1_, f32[2048,512]{1,0:T(8,128)} %collective-permute-done.16.refs_2_), custom_call_target="tpu_custom_call" | custom-call | flops 1048576 | bytes 20971520 | tf_op jit(solution)/shard_map/weave/pallas_call | solution.py:148
  (70 shorter events, 22.7 us)
Async XLA Ops:
  17.5 125.8 %all-to-all-start = ((bf16[16,208,512]{2,1,0:T(8,128)(2,1)}), bf16[16,208,512]{2,1,0:T(8,128)(2,1)}, u32[]{:S(2)}, u32[]{:S(2)}) async-start(bf16[16,208,512]{2,1,0:T(8,128)(2,1)} %flip.1), calls=%async_computation | async-start | bytes 6815744 | tf_op jit(solution)/shard_map/all_to_all | solution.py:221
  26.2 66.0 %all-gather.6.cloned.1.call-start = ((), (), s32[]{:S(2)}) async-start(), calls=%async_computation.4 | async-start | bytes 1310720 | tf_op jit(solution)/shard_map/all_gather | solution.py:230
  31.8 2.0 collective-permute-start
  35.7 264.7 %all-gather.4.cloned.1.call-start = ((), (), s32[]{:S(2)}) async-start(), calls=%async_computation.3 | async-start | bytes 3932160 | tf_op jit(solution)/shard_map/all_gather | solution.py:253
  92.2 34.0 %collective-permute-start.4 = (bf16[4,256,512]{2,1,0:T(8,128)(2,1)}, bf16[4,256,512]{2,1,0:T(8,128)(2,1)S(1)}, u32[]{:S(2)}, u32[]{:S(2)}) collective-permute-start(bf16[4,256,512]{2,1,0:T(8,128)(2,1)} %bitcast.55), channel_id=1, source_target_pairs={{0,16},{8,24},{16,0},{24,8},{1,17},{9,25},{17,1},{25,9},{2,18},{10... | collective-permute-start | bytes 3145736 | tf_op jit(solution)/shard_map/ppermute | solution.py:168
  93.7 34.1 %collective-permute-start.2 = (bf16[4,256,512]{2,1,0:T(8,128)(2,1)}, bf16[4,256,512]{2,1,0:T(8,128)(2,1)S(1)}, u32[]{:S(2)}, u32[]{:S(2)}) collective-permute-start(bf16[4,256,512]{2,1,0:T(8,128)(2,1)} %bitcast.56), channel_id=1, source_target_pairs={{0,8},{8,0},{16,24},{24,16},{1,9},{9,1},{17,25},{25,17},{2,10},{10... | collective-permute-start | bytes 3145736 | tf_op jit(solution)/shard_map/ppermute | solution.py:168
  126.2 22.0 %copy-start.3 = (bf16[4,256,512]{2,1,0:T(8,128)(2,1)}, bf16[4,256,512]{2,1,0:T(8,128)(2,1)S(1)}, u32[]{:S(2)}) copy-start(bf16[4,256,512]{2,1,0:T(8,128)(2,1)S(1)} %collective-permute-done.4.refs_9_) | copy-start | bytes 3145732
  126.3 12.9 %collective-permute-start.6 = (bf16[2,256,512]{2,1,0:T(8,128)(2,1)S(1)}, bf16[2,256,512]{2,1,0:T(8,128)(2,1)S(1)}, u32[]{:S(2)}, u32[]{:S(2)}) collective-permute-start(bf16[2,256,512]{2,1,0:T(8,128)(2,1)S(1)} %slice.62), channel_id=1, source_target_pairs={{0,8},{8,0},{16,24},{24,16},{1,9},{9,1},{17,25},{25,17},{2,10},{10... | collective-permute-start | bytes 1572872 | tf_op jit(solution)/shard_map/ppermute | solution.py:168
  127.8 20.4 %copy-start.4 = (bf16[4,256,512]{2,1,0:T(8,128)(2,1)}, bf16[4,256,512]{2,1,0:T(8,128)(2,1)S(1)}, u32[]{:S(2)}) copy-start(bf16[4,256,512]{2,1,0:T(8,128)(2,1)S(1)} %collective-permute-done.2.refs_7_) | copy-start | bytes 3145732
  127.9 12.9 %collective-permute-start.7 = (bf16[2,256,512]{2,1,0:T(8,128)(2,1)S(1)}, bf16[2,256,512]{2,1,0:T(8,128)(2,1)S(1)}, u32[]{:S(2)}, u32[]{:S(2)}) collective-permute-start(bf16[2,256,512]{2,1,0:T(8,128)(2,1)S(1)} %slice.63), channel_id=1, source_target_pairs={{0,16},{8,24},{16,0},{24,8},{1,17},{9,25},{17,1},{25,9},{2,18},{10... | collective-permute-start | bytes 1572872 | tf_op jit(solution)/shard_map/ppermute | solution.py:168
  128.5 19.7 %collective-permute-start.1 = (bf16[4,256,512]{2,1,0:T(8,128)(2,1)}, bf16[4,256,512]{2,1,0:T(8,128)(2,1)}, u32[]{:S(2)}, u32[]{:S(2)}) collective-permute-start(bf16[4,256,512]{2,1,0:T(8,128)(2,1)} %bitcast.57), channel_id=1, source_target_pairs={{0,1},{1,0},{2,3},{3,2},{4,5},{5,4},{6,7},{7,6},{8,9},{9,8},{10,11... | collective-permute-start | bytes 3145736 | tf_op jit(solution)/shard_map/ppermute | solution.py:171
  128.5 19.7 %collective-permute-start.5 = (bf16[4,256,512]{2,1,0:T(8,128)(2,1)S(1)}, bf16[4,256,512]{2,1,0:T(8,128)(2,1)}, u32[]{:S(2)}, u32[]{:S(2)}) collective-permute-start(bf16[4,256,512]{2,1,0:T(8,128)(2,1)S(1)} %collective-permute-done.4.refs_9_), channel_id=1, source_target_pairs={{0,1},{1,0},{2,3},{3,2},{4,5},{5,4},{6,7},{7,6},{8,9},{9,8},{10,11... | collective-permute-start | bytes 3145736 | tf_op jit(solution)/shard_map/ppermute | solution.py:171
  129.0 19.2 %collective-permute-start.3 = (bf16[4,256,512]{2,1,0:T(8,128)(2,1)S(1)}, bf16[4,256,512]{2,1,0:T(8,128)(2,1)}, u32[]{:S(2)}, u32[]{:S(2)}) collective-permute-start(bf16[4,256,512]{2,1,0:T(8,128)(2,1)S(1)} %collective-permute-done.2.refs_7_), channel_id=1, source_target_pairs={{0,1},{1,0},{2,3},{3,2},{4,5},{5,4},{6,7},{7,6},{8,9},{9,8},{10,11... | collective-permute-start | bytes 3145736 | tf_op jit(solution)/shard_map/ppermute | solution.py:171
  141.6 6.7 %collective-permute-start.8 = (bf16[4,256,512]{2,1,0:T(8,128)(2,1)}, bf16[4,256,512]{2,1,0:T(8,128)(2,1)}, u32[]{:S(2)}, u32[]{:S(2)}) collective-permute-start(bf16[4,256,512]{2,1,0:T(8,128)(2,1)} %constant_dynamic-update-slice_fusion.refs_11_), channel_id=1, source_target_pairs={{0,1},{1,0},{2,3},{3,2},{4,5},{5,4},{6,7},{7,6},{8,9},{9,8},{10,11... | collective-permute-start | bytes 3145736 | tf_op jit(solution)/shard_map/ppermute | solution.py:171
  175.6 32.1 %collective-permute-start.10 = (bf16[768,512]{1,0:T(8,128)(2,1)S(1)}, bf16[768,512]{1,0:T(8,128)(2,1)S(1)}, u32[]{:S(2)}, u32[]{:S(2)}) collective-permute-start(bf16[768,512]{1,0:T(8,128)(2,1)S(1)} %bitcast.49), channel_id=1, source_target_pairs={{2,0},{4,2},{6,4},{3,1},{5,3},{7,5},{10,8},{12,10},{14,12},{11,9},... | collective-permute-start | bytes 2359304 | tf_op jit(solution)/shard_map/ppermute | solution.py:190
  176.9 30.8 %collective-permute-start.9 = (bf16[768,512]{1,0:T(8,128)(2,1)S(1)}, bf16[768,512]{1,0:T(8,128)(2,1)S(1)}, u32[]{:S(2)}, u32[]{:S(2)}) collective-permute-start(bf16[768,512]{1,0:T(8,128)(2,1)S(1)} %bitcast.50), channel_id=1, source_target_pairs={{0,2},{2,4},{4,6},{1,3},{3,5},{5,7},{8,10},{10,12},{12,14},{9,11},... | collective-permute-start | bytes 2359304 | tf_op jit(solution)/shard_map/ppermute | solution.py:189
  207.8 23.4 %collective-permute-start.11 = (bf16[768,512]{1,0:T(8,128)(2,1)S(1)}, bf16[768,512]{1,0:T(8,128)(2,1)S(1)}, u32[]{:S(2)}, u32[]{:S(2)}) collective-permute-start(bf16[768,512]{1,0:T(8,128)(2,1)S(1)} %collective-permute-done.10), channel_id=1, source_target_pairs={{2,0},{4,2},{3,1},{5,3},{10,8},{12,10},{11,9},{13,11},{18,16},{20,... | collective-permute-start | bytes 2359304 | tf_op jit(solution)/shard_map/ppermute | solution.py:190
  209.1 23.4 %collective-permute-start.13 = (bf16[768,512]{1,0:T(8,128)(2,1)S(1)}, bf16[768,512]{1,0:T(8,128)(2,1)}, u32[]{:S(2)}, u32[]{:S(2)}) collective-permute-start(bf16[768,512]{1,0:T(8,128)(2,1)S(1)} %collective-permute-done.9), channel_id=1, source_target_pairs={{2,4},{4,6},{3,5},{5,7},{10,12},{12,14},{11,13},{13,15},{18,20},{2... | collective-permute-start | bytes 2359304 | tf_op jit(solution)/shard_map/ppermute | solution.py:189
  231.2 30.8 %collective-permute-start.12 = (bf16[768,512]{1,0:T(8,128)(2,1)S(1)}, bf16[768,512]{1,0:T(8,128)(2,1)}, u32[]{:S(2)}, u32[]{:S(2)}) collective-permute-start(bf16[768,512]{1,0:T(8,128)(2,1)S(1)} %collective-permute-done.11), channel_id=1, source_target_pairs={{2,0},{3,1},{10,8},{11,9},{18,16},{19,17},{26,24},{27,25}} | collective-permute-start | bytes 2359304 | tf_op jit(solution)/shard_map/ppermute | solution.py:190
  232.5 31.2 %collective-permute-start.14 = (bf16[768,512]{1,0:T(8,128)(2,1)}, bf16[768,512]{1,0:T(8,128)(2,1)}, u32[]{:S(2)}, u32[]{:S(2)}) collective-permute-start(bf16[768,512]{1,0:T(8,128)(2,1)} %collective-permute-done.13), channel_id=1, source_target_pairs={{4,6},{5,7},{12,14},{13,15},{20,22},{21,23},{28,30},{29,31}} | collective-permute-start | bytes 2359304 | tf_op jit(solution)/shard_map/ppermute | solution.py:189
  264.0 12.2 %copy-start.1 = (bf16[4,768,512]{2,1,0:T(8,128)(2,1)}, bf16[4,768,512]{2,1,0:T(8,128)(2,1)S(1)}, u32[]{:S(2)}) copy-start(bf16[4,768,512]{2,1,0:T(8,128)(2,1)S(1)} %bitcast_dynamic-update-slice_fusion) | copy-start | bytes 9437188
  276.2 24.2 %collective-permute-start.15 = (f32[2048,512]{1,0:T(8,128)}, f32[2048,512]{1,0:T(8,128)}, u32[]{:S(2)}, u32[]{:S(2)}) collective-permute-start(f32[2048,512]{1,0:T(8,128)} %fusion.2), channel_id=1, source_target_pairs={{0,1},{1,0},{2,3},{3,2},{4,5},{5,4},{6,7},{7,6},{8,9},{9,8},{10,11... | collective-permute-start | bytes 12582920 | tf_op jit(solution)/shard_map/ppermute | solution.py:269
  300.4 14.9 %copy-start.7 = (bf16[3072,512]{1,0:T(8,128)(2,1)S(1)}, bf16[3072,512]{1,0:T(8,128)(2,1)}, u32[]{:S(2)}) copy-start(bf16[3072,512]{1,0:T(8,128)(2,1)} %all-gather.4.cloned.1.call-done) | copy-start | bytes 9437188
  325.0 11.1 %collective-permute-start.16 = (f32[2048,512]{1,0:T(8,128)S(1)}, f32[2048,512]{1,0:T(8,128)}, u32[]{:S(2)}, u32[]{:S(2)}) collective-permute-start(f32[2048,512]{1,0:T(8,128)S(1)} %fusion), channel_id=1, source_target_pairs={{0,1},{1,0},{2,3},{3,2},{4,5},{5,4},{6,7},{7,6},{8,9},{9,8},{10,11... | collective-permute-start | bytes 12582920 | tf_op jit(solution)/shard_map/ppermute | solution.py:269
  (4 other events, 10.8 us)
Sparse Core Ops, SparseCore 0:
  35.8 56.3 all-gather.5
  234.2 66.1 all-gather.3
